TPU v7x, 256 devices: a whole 4x4x8 slice. The times are simulated.
256 devices in a mesh: tm: 32 (over x_lo, z, core), tile: 8 (over x_hi, y).
Axes of the slice: x: 4 (x_hi: 2, x_lo: 2; x = x_hi * 2 + x_lo), y: 4, z: 8, core: 2. Of those that a mesh axis runs over, the one named last changes fastest.
Arguments:
- queries: bfloat16 [64, 16, 64, 2560], P('tm', 'tile'), may hold values from -40 to 40
- keys: bfloat16 [64, 16, 64, 2560], P('tm', 'tile'), may hold values from -6 to 6
- values: bfloat16 [64, 16, 64, 2560], P('tm', 'tile'), may hold values from -6 to 6
- neighbours: int32 [32, 8, 3], P('tm', 'tile'), may hold values from -1 to 30, as said below
- halo_rows: int32 [32, 8], P('tm', 'tile'), may hold values from 0 to 2, as said below
Outputs:
- attended: bfloat16 [64, 16, 64, 2560], P('tm', 'tile')
Inputs may be any that keep to these rules, and one draw needn't show every extreme that they name: `neighbours`: for frame block b and tile t, the entries that are not -1 are distinct frame blocks from max(0, b - 5) to b - 1; lists hold 0 to 3 entries, and some list is full. `halo_rows`: some frame block and tile reads 2 rows.
All inputs are finite; a program needn't handle non-finite values.
Results may differ from a plain program's by a relative error of at most 0.0046.
Values may be sent and summed in bfloat16 or wider, within the bound.
A program may use at most 128 MiB of HBM per device.

v0:
```python
import math

import jax
import jax.numpy as jnp
from jax import lax
from jax.sharding import PartitionSpec as P

HD = 128
HMAX = 2
WIN = 5


def padded_2(x, sides, width):
    for axis, dim in sides:
        size, length = (lax.axis_size(axis), x.shape[dim])
        up = [(i, (i + 1) % size) for i in range(size - 1)]
        down = [(j, i) for i, j in up]
        last = lax.slice_in_dim(x, length - width, length, axis=dim)
        leading = lax.slice_in_dim(x, 0, width, axis=dim)
        before = lax.ppermute(last, axis, up)
        after = lax.ppermute(leading, axis, down)
        x = jnp.concatenate([before, x, after], axis=dim)
    return x


def from_behind(value, axis, steps):
    count = lax.axis_size(axis)
    leading, last = (max(0, -steps), min(count, count - steps))
    return lax.ppermute(value, axis, [(source, source + steps) for source in range(leading, last)])


def head_groups(query_rows, key_rows, value_rows, allowed):
    tokens, channels = query_rows.shape
    head_count = channels // HD
    key_count = key_rows.shape[0]
    group_size = 2
    group_count = head_count // group_size
    columns = group_size * HD

    def one_group(group_index):
        offset = group_index * columns
        query_part = lax.dynamic_slice_in_dim(query_rows, offset, columns, 1).reshape(
            tokens, group_size, HD
        )
        key_part = lax.dynamic_slice_in_dim(key_rows, offset, columns, 1).reshape(
            key_count, group_size, HD
        )
        value_part = lax.dynamic_slice_in_dim(value_rows, offset, columns, 1).reshape(
            key_count, group_size, HD
        )
        scores = jnp.einsum(
            "qhd,khd->hqk", query_part, key_part, preferred_element_type=jnp.float32
        ) / math.sqrt(HD)
        scores = jnp.where(allowed[None], scores, -jnp.inf)
        maximum = jnp.max(scores, axis=2, keepdims=True)
        weights = jnp.where(allowed[None], jnp.exp(scores - maximum), 0.0)
        totals = jnp.sum(weights, axis=2)
        numerator = jnp.einsum(
            "hqk,khd->qhd",
            weights.astype(jnp.bfloat16),
            value_part,
            preferred_element_type=jnp.float32,
        )
        return (numerator / totals.T[:, :, None]).reshape(tokens, columns).astype(jnp.bfloat16)

    pieces = lax.map(one_group, jnp.arange(group_count, dtype=jnp.int32))
    return pieces.transpose(1, 0, 2).reshape(tokens, channels)


def local(queries, keys, values, neighbours, halo_rows):
    frames, tile_rows, grid_columns, channels = queries.shape
    tokens = frames * tile_rows * grid_columns
    span_rows = tile_rows + 2 * HMAX
    block_index = lax.axis_index("tm")
    tile_index = lax.axis_index("tile")
    tile_count = lax.axis_size("tile")
    key_value = jnp.stack((keys, values))
    padded = padded_2(key_value, (("tile", 2),), HMAX)
    moving = key_value
    earlier = []
    for hop_number in range(WIN):
        moving = from_behind(moving, "tm", 1)
        earlier.append(moving)
    stacked = jnp.stack(earlier)
    listed = neighbours[0, 0]
    halo_reach = halo_rows[0, 0]
    position = jnp.clip(block_index - listed - 1, 0, WIN - 1)
    chosen = jnp.take(stacked, position, axis=0)
    present = listed >= 0
    query_frame = lax.broadcasted_iota(jnp.int32, (frames, tile_rows, grid_columns), 0).reshape(-1)
    key_frame = lax.broadcasted_iota(jnp.int32, (frames, span_rows, grid_columns), 0).reshape(-1)
    key_row = lax.broadcasted_iota(jnp.int32, (frames, span_rows, grid_columns), 1).reshape(-1)
    global_row = tile_index * tile_rows - HMAX + key_row
    row_ok = (
        (global_row >= 0)
        & (global_row < tile_rows * tile_count)
        & (key_row >= HMAX - halo_reach)
        & (key_row < HMAX + tile_rows + halo_reach)
    )
    own_mask = (key_frame[None, :] <= query_frame[:, None]) & row_ok[None, :]
    slot_mask = jnp.repeat(present, tokens)
    allowed = jnp.concatenate(
        (own_mask, jnp.broadcast_to(slot_mask[None, :], (tokens, slot_mask.shape[0]))), axis=1
    )
    key_rows = jnp.concatenate(
        (padded[0].reshape(-1, channels), chosen[:, 0].reshape(-1, channels)), axis=0
    )
    value_rows = jnp.concatenate(
        (padded[1].reshape(-1, channels), chosen[:, 1].reshape(-1, channels)), axis=0
    )
    result = head_groups(queries.reshape(tokens, channels), key_rows, value_rows, allowed)
    return result.reshape(frames, tile_rows, grid_columns, channels)


def solution(mesh):
    return jax.shard_map(
        local,
        mesh=mesh,
        in_specs=(
            P("tm", "tile", None, None),
            P("tm", "tile", None, None),
            P("tm", "tile", None, None),
            P("tm", "tile", None),
            P("tm", "tile"),
        ),
        out_specs=P("tm", "tile", None, None),
        check_vma=False,
    )
```

profile of v0, /device:TPU:56, one launch (start us, length us, event | category | flops | bytes accessed | tf_op | source)
XLA Modules:
  0.0 416.0 jit_solution(2411673498480911605)
XLA Ops:
  0.0 3.6 pad_maximum_fusion.3
  3.6 1.9 collective-permute-start.2
  5.5 31.3 %collective-permute-done.2 = bf16[2,2,2,64,2560]{4,3,2,1,0:T(8,128)(2,1)S(1)} collective-permute-done((bf16[2,2,2,64,2560]{4,3,2,1,0:T(8,128)(2,1)}, bf16[2,2,2,64,2560]{4,3,2,1,0:T(8,128)(2,1)S(1)}, u32[]{:S(2)}, u32[]{:S(2)}) %collective-permute-start.2) | collective-permute-done | bytes 2621472 | tf_op jit(solution)/shard_map/ppermute | solution.py:29
  36.8 1.5 copy-done.2
  38.3 1.9 collective-permute-start.3
  40.2 31.1 %collective-permute-done.3 = bf16[2,2,2,64,2560]{4,3,2,1,0:T(8,128)(2,1)} collective-permute-done((bf16[2,2,2,64,2560]{4,3,2,1,0:T(8,128)(2,1)S(1)}, bf16[2,2,2,64,2560]{4,3,2,1,0:T(8,128)(2,1)}, u32[]{:S(2)}, u32[]{:S(2)}) %collective-permute-start.3) | collective-permute-done | bytes 2621472 | tf_op jit(solution)/shard_map/ppermute | solution.py:29
  71.4 1.9 collective-permute-start.4
  73.3 4.6 %collective-permute-start = (bf16[2,2,2,64,2560]{4,3,2,1,0:T(8,128)(2,1)}, bf16[2,2,2,64,2560]{4,3,2,1,0:T(8,128)(2,1)}, u32[]{:S(2)}, u32[]{:S(2)}) collective-permute-start(bf16[2,2,2,64,2560]{4,3,2,1,0:T(8,128)(2,1)} %pad_maximum_fusion.3), channel_id=1, source_target_pairs={{0,1},{1,2},{2,3},{3,4},{4,5},{5,6},{6,7},{8,9},{9,10},{10,11},{11... | collective-permute-start | bytes 7864328 | tf_op jit(solution)/shard_map/ppermute | solution.py:20
  77.9 1.9 collective-permute-start.1
  80.6 24.1 %collective-permute-done.4 = bf16[2,2,2,64,2560]{4,3,2,1,0:T(8,128)(2,1)} collective-permute-done((bf16[2,2,2,64,2560]{4,3,2,1,0:T(8,128)(2,1)}, bf16[2,2,2,64,2560]{4,3,2,1,0:T(8,128)(2,1)}, u32[]{:S(2)}, u32[]{:S(2)}) %collective-permute-start.4) | collective-permute-done | bytes 2621472 | tf_op jit(solution)/shard_map/ppermute | solution.py:29
  104.7 1.9 collective-permute-start.5
  107.3 27.1 %collective-permute-done = bf16[2,2,2,64,2560]{4,3,2,1,0:T(8,128)(2,1)} collective-permute-done((bf16[2,2,2,64,2560]{4,3,2,1,0:T(8,128)(2,1)}, bf16[2,2,2,64,2560]{4,3,2,1,0:T(8,128)(2,1)}, u32[]{:S(2)}, u32[]{:S(2)}) %collective-permute-start) | collective-permute-done | bytes 2621472 | tf_op jit(solution)/shard_map/ppermute | solution.py:20
  134.4 8.3 %collective-permute-done.1 = bf16[2,2,2,64,2560]{4,3,2,1,0:T(8,128)(2,1)} collective-permute-done((bf16[2,2,2,64,2560]{4,3,2,1,0:T(8,128)(2,1)}, bf16[2,2,2,64,2560]{4,3,2,1,0:T(8,128)(2,1)}, u32[]{:S(2)}, u32[]{:S(2)}) %collective-permute-start.1) | collective-permute-done | bytes 2621472 | tf_op jit(solution)/shard_map/ppermute | solution.py:21
  142.7 3.5 pad_maximum_fusion
  146.3 3.4 fusion.32
  149.7 2.7 collective-permute-start.6
  152.4 1.7 bitcast_dynamic-update-slice_fusion.4
  154.1 6.3 %copy.18 = bf16[768,2560]{0,1:T(8,128)(2,1)} copy(bf16[768,2560]{1,0:T(8,128)(2,1)} %bitcast.72) | data formatting | bytes 7864320 | tf_op jit(solution)/shard_map/reshape;squeeze | solution.py:106
  160.4 3.4 bitcast_dynamic-update-slice_fusion.3
  163.8 3.4 bitcast_dynamic-update-slice_fusion.2
  167.2 3.5 bitcast_dynamic-update-slice_fusion.1
  170.6 94.5 %collective-permute-done.6 = bf16[2,2,2,64,2560]{4,3,2,1,0:T(8,128)(2,1)S(1)} collective-permute-done((bf16[2,2,2,64,2560]{4,3,2,1,0:T(8,128)(2,1)}, bf16[2,2,2,64,2560]{4,3,2,1,0:T(8,128)(2,1)S(1)}, u32[]{:S(2)}, u32[]{:S(2)}) %collective-permute-start.6) | collective-permute-done | bytes 2621472 | tf_op jit(solution)/shard_map/ppermute | solution.py:29
  265.2 1.8 bitcast_dynamic-update-slice_fusion
  267.0 9.8 %fusion.31 = (bf16[5,2,2,2,64,1280]{5,4,3,2,1,0:T(8,128)(2,1)}, bf16[5,2,2,2,64,1280]{5,4,3,2,1,0:T(8,128)(2,1)}) fusion(bf16[5,2,2,2,64,2560]{5,4,3,2,1,0:T(8,128)(2,1)} %bitcast_dynamic-update-slice_fusion), kind=kLoop, calls=%fused_computation.51 | loop fusion | bytes 26214400 | tf_op jit(solution)/shard_map/jit(_take)/gather | solution.py:88
  276.7 5.8 %gather_fusion = bf16[3,2,2,2,64,1280]{5,4,3,2,1,0:T(8,128)(2,1)} fusion(bf16[5,2,2,2,64,1280]{5,4,3,2,1,0:T(8,128)(2,1)} %get-tuple-element.71, s32[1024]{0:T(1024)S(1)} %pad_clamp_fusion), kind=kCustom, calls=%fused_computation | custom fusion | bytes 7864332 | tf_op jit(solution)/shard_map/jit(_take)/gather | solution.py:88
  282.5 5.7 %gather_fusion.1 = bf16[3,2,2,2,64,1280]{5,4,3,2,1,0:T(8,128)(2,1)} fusion(bf16[5,2,2,2,64,1280]{5,4,3,2,1,0:T(8,128)(2,1)} %get-tuple-element.72, s32[1024]{0:T(1024)S(1)} %pad_clamp_fusion), kind=kCustom, calls=%fused_computation.1 | custom fusion | bytes 7864332 | tf_op jit(solution)/shard_map/jit(_take)/gather | solution.py:88
  288.2 8.3 %maximum_select_fusion = bf16[3,2,2,2,64,2560]{5,4,3,2,1,0:T(8,128)(2,1)} fusion(bf16[3,2,2,2,64,1280]{5,4,3,2,1,0:T(8,128)(2,1)} %gather_fusion.1, bf16[3,2,2,2,64,1280]{5,4,3,2,1,0:T(8,128)(2,1)} %gather_fusion, pred[3]{0:T(512)(128)(4,1)S(1)} %compare_and_fusion.1), kind=kLoop, calls=%fused_computation.24 | loop fusion | flops 19660800 | bytes 15728643 | tf_op jit(solution)/shard_map/jit(_take)/select_n | solution.py:88
  296.5 5.4 %fusion.33 = (bf16[3,1,2,2,64,2560]{5,4,3,2,1,0:T(8,128)(2,1)}, bf16[3,1,2,2,64,2560]{5,4,3,2,1,0:T(8,128)(2,1)}) fusion(bf16[3,2,2,2,64,2560]{5,4,3,2,1,0:T(8,128)(2,1)} %maximum_select_fusion), kind=kLoop, calls=%fused_computation.53 | loop fusion | bytes 15728640 | tf_op jit(solution)/shard_map/slice | solution.py:106
  301.9 6.2 %copy.19 = bf16[768,2560]{0,1:T(8,128)(2,1)} copy(bf16[768,2560]{1,0:T(8,128)(2,1)} %bitcast.73) | data formatting | bytes 7864320 | tf_op jit(solution)/shard_map/reshape;squeeze | solution.py:106
  308.1 6.9 %pad_maximum_fusion.2 = bf16[1536,2560]{0,1:T(8,128)(2,1)} fusion(bf16[768,2560]{0,1:T(8,128)(2,1)} %copy.19, bf16[768,2560]{0,1:T(8,128)(2,1)} %copy.18), kind=kLoop, calls=%fused_computation.26 | loop fusion | flops 15728640 | bytes 15728640 | tf_op jit(solution)/shard_map/concatenate | solution.py:105
  315.0 7.0 %pad_maximum_fusion.1 = bf16[1536,2560]{1,0:T(8,128)(2,1)} fusion(bf16[768,2560]{1,0:T(8,128)(2,1)} %bitcast.75, bf16[768,2560]{1,0:T(8,128)(2,1)} %bitcast.74), kind=kLoop, calls=%fused_computation.25 | loop fusion | flops 15728640 | bytes 15728640 | tf_op jit(solution)/shard_map/concatenate | solution.py:108
  322.0 88.9 %while.10 = (s32[]{:T(128)}, bf16[10,256,256]{1,2,0:T(8,128)(2,1)}, s32[10]{0:T(128)S(1)}, bf16[1536,2560]{1,0:T(8,128)(2,1)}, pred[256,1536]{1,0:T(8,128)(4,1)S...) while((s32[]{:T(128)}, bf16[10,256,256]{1,2,0:T(8,128)(2,1)}, ...), condition=%wide.region_3.4_spmd, body=%wide.region_0.0_spmd.sunk | while | flops 611978752 | bytes 9048755 | solution.py:66
  325.4 1.6 fusion.53
  327.1 1.2 constant_dynamic-slice_fusion.6
  328.6 1.6 fusion.54
  334.3 1.6 fusion.53
  336.0 1.2 constant_dynamic-slice_fusion.6
  337.4 1.6 fusion.54
  343.2 1.6 fusion.53
  344.9 1.2 constant_dynamic-slice_fusion.6
  346.3 1.6 fusion.54
  352.1 1.6 fusion.53
  353.7 1.2 constant_dynamic-slice_fusion.6
  355.2 1.6 fusion.54
  361.0 1.6 fusion.53
  362.6 1.2 constant_dynamic-slice_fusion.6
  364.1 1.6 fusion.54
  369.9 1.6 fusion.53
  371.5 1.2 constant_dynamic-slice_fusion.6
  373.0 1.6 fusion.54
  378.8 1.6 fusion.53
  380.4 1.2 constant_dynamic-slice_fusion.6
  381.9 1.6 fusion.54
  387.6 1.6 fusion.53
  389.3 1.2 constant_dynamic-slice_fusion.6
  390.8 1.6 fusion.54
  396.5 1.6 fusion.53
  398.2 1.2 constant_dynamic-slice_fusion.6
  399.6 1.6 fusion.54
  405.4 1.6 fusion.53
  407.0 1.2 constant_dynamic-slice_fusion.6
  408.5 1.6 fusion.54
  410.8 3.5 copy.22
  414.3 1.7 reshape_reshape.3
  (87 shorter events, 38.4 us)
Async XLA Ops:
  0.0 142.7 %copy-start.1 = (bf16[2,2,64,2560]{3,2,1,0:T(8,128)(2,1)S(1)}, bf16[2,2,64,2560]{3,2,1,0:T(8,128)(2,1)}, u32[]{:S(2)}) copy-start(bf16[2,2,64,2560]{3,2,1,0:T(8,128)(2,1)} %param.8) | copy-start | bytes 3932164
  0.0 142.7 %copy-start = (bf16[2,2,64,2560]{3,2,1,0:T(8,128)(2,1)S(1)}, bf16[2,2,64,2560]{3,2,1,0:T(8,128)(2,1)}, u32[]{:S(2)}) copy-start(bf16[2,2,64,2560]{3,2,1,0:T(8,128)(2,1)} %param.9) | copy-start | bytes 3932164
  0.0 80.5 %copy-start.4 = (s32[1,1,3]{2,1,0:T(1,128)S(1)}, s32[1,1,3]{2,1,0:T(1,128)}, u32[]{:S(2)}) copy-start(s32[1,1,3]{2,1,0:T(1,128)} %param.10) | copy-start | bytes 40
  3.6 33.2 %collective-permute-start.2 = (bf16[2,2,2,64,2560]{4,3,2,1,0:T(8,128)(2,1)}, bf16[2,2,2,64,2560]{4,3,2,1,0:T(8,128)(2,1)S(1)}, u32[]{:S(2)}, u32[]{:S(2)}) collective-permute-start(bf16[2,2,2,64,2560]{4,3,2,1,0:T(8,128)(2,1)} %pad_maximum_fusion.3), channel_id=1, source_target_pairs={{0,8},{8,16},{16,24},{24,32},{32,40},{40,48},{48,56},{56,64},{64,7... | collective-permute-start | bytes 7864328 | tf_op jit(solution)/shard_map/ppermute | solution.py:29
  36.8 1.5 copy-start.2
  38.3 33.1 %collective-permute-start.3 = (bf16[2,2,2,64,2560]{4,3,2,1,0:T(8,128)(2,1)S(1)}, bf16[2,2,2,64,2560]{4,3,2,1,0:T(8,128)(2,1)}, u32[]{:S(2)}, u32[]{:S(2)}) collective-permute-start(bf16[2,2,2,64,2560]{4,3,2,1,0:T(8,128)(2,1)S(1)} %collective-permute-done.2), channel_id=1, source_target_pairs={{0,8},{8,16},{16,24},{24,32},{32,40},{40,48},{48,56},{56,64},{64,7... | collective-permute-start | bytes 7864328 | tf_op jit(solution)/shard_map/ppermute | solution.py:29
  71.4 33.3 %collective-permute-start.4 = (bf16[2,2,2,64,2560]{4,3,2,1,0:T(8,128)(2,1)}, bf16[2,2,2,64,2560]{4,3,2,1,0:T(8,128)(2,1)}, u32[]{:S(2)}, u32[]{:S(2)}) collective-permute-start(bf16[2,2,2,64,2560]{4,3,2,1,0:T(8,128)(2,1)} %collective-permute-done.3), channel_id=1, source_target_pairs={{0,8},{8,16},{16,24},{24,32},{32,40},{40,48},{48,56},{56,64},{64,7... | collective-permute-start | bytes 7864328 | tf_op jit(solution)/shard_map/ppermute | solution.py:29
  73.3 61.1 %collective-permute-start = (bf16[2,2,2,64,2560]{4,3,2,1,0:T(8,128)(2,1)}, bf16[2,2,2,64,2560]{4,3,2,1,0:T(8,128)(2,1)}, u32[]{:S(2)}, u32[]{:S(2)}) collective-permute-start(bf16[2,2,2,64,2560]{4,3,2,1,0:T(8,128)(2,1)} %pad_maximum_fusion.3), channel_id=1, source_target_pairs={{0,1},{1,2},{2,3},{3,4},{4,5},{5,6},{6,7},{8,9},{9,10},{10,11},{11... | collective-permute-start | bytes 7864328 | tf_op jit(solution)/shard_map/ppermute | solution.py:20
  77.9 64.8 %collective-permute-start.1 = (bf16[2,2,2,64,2560]{4,3,2,1,0:T(8,128)(2,1)}, bf16[2,2,2,64,2560]{4,3,2,1,0:T(8,128)(2,1)}, u32[]{:S(2)}, u32[]{:S(2)}) collective-permute-start(bf16[2,2,2,64,2560]{4,3,2,1,0:T(8,128)(2,1)} %pad_maximum_fusion.3), channel_id=1, source_target_pairs={{1,0},{2,1},{3,2},{4,3},{5,4},{6,5},{7,6},{9,8},{10,9},{11,10},{12... | collective-permute-start | bytes 7864328 | tf_op jit(solution)/shard_map/ppermute | solution.py:21
  104.7 45.0 %collective-permute-start.5 = (bf16[2,2,2,64,2560]{4,3,2,1,0:T(8,128)(2,1)}, bf16[2,2,2,64,2560]{4,3,2,1,0:T(8,128)(2,1)}, u32[]{:S(2)}, u32[]{:S(2)}) collective-permute-start(bf16[2,2,2,64,2560]{4,3,2,1,0:T(8,128)(2,1)} %collective-permute-done.4), channel_id=1, source_target_pairs={{0,8},{8,16},{16,24},{24,32},{32,40},{40,48},{48,56},{56,64},{64,7... | collective-permute-start | bytes 7864328 | tf_op jit(solution)/shard_map/ppermute | solution.py:29
  146.2 6.1 %copy-start.3 = (bf16[2,2,2,64,2560]{4,3,2,1,0:T(8,128)(2,1)S(1)}, bf16[2,2,2,64,2560]{4,3,2,1,0:T(8,128)(2,1)}, u32[]{:S(2)}) copy-start(bf16[2,2,2,64,2560]{4,3,2,1,0:T(8,128)(2,1)} %copy-done.2) | copy-start | bytes 7864324
  149.7 115.5 %collective-permute-start.6 = (bf16[2,2,2,64,2560]{4,3,2,1,0:T(8,128)(2,1)}, bf16[2,2,2,64,2560]{4,3,2,1,0:T(8,128)(2,1)S(1)}, u32[]{:S(2)}, u32[]{:S(2)}) collective-permute-start(bf16[2,2,2,64,2560]{4,3,2,1,0:T(8,128)(2,1)} %collective-permute-done.5), channel_id=1, source_target_pairs={{0,8},{8,16},{16,24},{24,32},{32,40},{40,48},{48,56},{56,64},{64,7... | collective-permute-start | bytes 7864328 | tf_op jit(solution)/shard_map/ppermute | solution.py:29
where the time goes:
time: 418 us; the launch traced here: 416 us
  waiting for transfers between devices  216 us (52%)
  local copies, waits for them, and re-layouts  113 us (27%)
  matrix products  32.6 us (8%)
  other arithmetic  29.7 us (7%)
  starting transfers between devices  16.8 us (4%)
  loops' own time  6.73 us (2%)
    ppermute x5, waiting for transfers between devices, from_behind(): lax.ppermute(value, axis, [(source, source + steps) for source in range(l...  181 us
    ppermute x1, waiting for transfers between devices, padded_2(): before = lax.ppermute(last, axis, up)  27.1 us
    gather x3, local copies, waits for them, and re-layouts, local(): chosen = jnp.take(stacked, position, axis=0)  21.2 us
    sub x10, matrix products, one_group(): weights = jnp.where(allowed[None], jnp.exp(scores - maximum), 0.0)  16.4 us
    dot_general x10, matrix products, one_group(): jnp.einsum('hqk,khd->qhd', weights.astype(jnp.bfloat16), value_part, pref...  16.3 us
    dynamic_slice x20, local copies, waits for them, and re-layouts, one_group(): lax.dynamic_slice_in_dim(value_rows, offset, columns, 1)  14.7 us
    unnamed x14, local copies, waits for them, and re-layouts  13.5 us
    dynamic_slice x10, local copies, waits for them, and re-layouts, one_group(): lax.dynamic_slice_in_dim(key_rows, offset, columns, 1)  11.9 us
  transfers between devices with their start and end apart: 7, of which 6 were waited for; matrix products, arithmetic and copies ran while one was open for 6% of the time, Pallas kernels for 0%

commit v1 on v0

v1 whole, which is shorter than its diff:
```python
import functools
import math

import jax
import jax.numpy as jnp
from jax import lax
from jax.experimental import pallas as pl
from jax.experimental.pallas import tpu as pltpu
from jax.sharding import PartitionSpec as P

HD = 128
WIN = 5
BIG = 1e30
SCALE = math.log2(math.e) / math.sqrt(HD)
LAGS = (1, 2, 3, 4, 5, 6)
MESH = pl.DeviceIdType.MESH


def attend(parts):
    top = None
    for scores, _, groups in parts:
        for start, size, seen in groups:
            peak = jnp.max(scores[start : start + size], axis=0, keepdims=True)
            peak = jnp.where(seen, peak, -BIG)
            top = peak if top is None else jnp.maximum(top, peak)
    total, out = None, None
    for scores, value_t, groups in parts:
        pieces = []
        for start, size, seen in groups:
            shift = jnp.where(seen, top, BIG)
            weights = jnp.exp2((scores[start : start + size] - shift) * SCALE)
            added = jnp.sum(weights, axis=0, keepdims=True)
            total = added if total is None else total + added
            pieces.append(weights.astype(jnp.bfloat16))
        weights = pieces[0] if len(pieces) == 1 else jnp.concatenate(pieces, axis=0)
        product = jnp.dot(value_t, weights, preferred_element_type=jnp.float32)
        out = product if out is None else out + product
    return out, total, top


def scores_of(keys, queries):
    return lax.dot_general(
        keys, queries, (((1,), (1,)), ((), ())), preferred_element_type=jnp.float32
    )


def settle(total, top):
    empty = total == 0.0
    lse = jnp.where(empty, -BIG, top * SCALE + jnp.log2(jnp.where(empty, 1.0, total)))
    return lse, 1.0 / jnp.where(empty, 1.0, total)


def merge(lse_a, lse_b):
    top = jnp.maximum(lse_a, lse_b)
    wa, wb = jnp.exp2(lse_a - top), jnp.exp2(lse_b - top)
    both = wa + wb
    return wa / both, wb / both, top + jnp.log2(both)


def kernel(
    blocks,
    tiles,
    heads,
    q_ref,
    k_ref,
    v_ref,
    meta_ref,
    out_ref,
    qo,
    kvo,
    kvh,
    vt,
    vth,
    rq,
    ro,
    rl,
    so,
    sl,
    outs,
    om,
    rm,
    q_local,
    q_remote,
    kv_sem,
    meta_sem,
    halo_sem,
    m_sem,
    n_sem,
    l_sem,
    m_sent,
    n_sent,
    l_sent,
    x_sent,
    halo_sent,
    out_sem,
):
    chunks = 2 * heads
    me = lax.axis_index("tm")
    tile = lax.axis_index("tile")
    core = lax.rem(me, 2)
    other = 1 - core
    partner = {"tm": me + 1 - 2 * core}
    back = {"tm": lax.rem(me + blocks - 2, blocks)}
    ahead = {"tm": lax.rem(me + 2, blocks)}
    up = {"tile": lax.max(tile - 1, 0)}
    down = {"tile": lax.min(tile + 1, tiles - 1)}
    has_up = tile > 0
    has_down = tile < tiles - 1

    def remote(src, dst, sent, received, device):
        return pltpu.make_async_remote_copy(
            src_ref=src,
            dst_ref=dst,
            send_sem=sent,
            recv_sem=received,
            device_id=device,
            device_id_type=MESH,
        )

    def arrived(ref, sem):
        pltpu.make_async_copy(ref, ref, sem).wait()

    def column(half, h):
        return pl.ds(pl.multiple_of((half * heads + h) * HD, HD), HD)

    barrier = pltpu.get_barrier_semaphore()
    rings = ({"tile": lax.rem(tile + 1, tiles)}, {"tile": lax.rem(tile + tiles - 1, tiles)})
    for device in (partner, back, ahead) + rings:
        pl.semaphore_signal(barrier, inc=1, device_id=device, device_id_type=MESH)

    pltpu.make_async_copy(meta_ref, om.at[core], meta_sem.at[0]).start()

    def fetch_q(h, _):
        pltpu.make_async_copy(
            q_ref.at[:, :, column(core, h)], qo.at[h, :, core], q_local.at[h]
        ).start()
        return 0

    def fetch_kv(h, _):
        for i, ref in enumerate((k_ref, v_ref)):
            pltpu.make_async_copy(
                ref.at[:, column(core, h)], kvo.at[h, i, core], kv_sem.at[0]
            ).start()
        return 0

    lax.fori_loop(0, heads, fetch_q, 0)
    lax.fori_loop(0, heads, fetch_kv, 0)

    pl.semaphore_wait(barrier, 5)

    remote(meta_ref, om.at[core], x_sent.at[0], meta_sem.at[1], partner).start()

    def give_q(h, _):
        remote(
            q_ref.at[:, :, column(other, h)], qo.at[h, :, core], x_sent.at[1], q_remote.at[h], partner
        ).start()
        return 0

    def give_kv(h, _):
        for i, ref in enumerate((k_ref, v_ref)):
            remote(
                ref.at[:, column(other, h)], kvo.at[h, i, core], x_sent.at[2], kv_sem.at[1], partner
            ).start()
        return 0

    lax.fori_loop(0, heads, give_q, 0)
    lax.fori_loop(0, heads, give_kv, 0)

    @pl.when(jnp.logical_not(has_up))
    def _():
        def clear(h, _):
            kvh[0, h] = jnp.zeros(kvh.shape[2:], kvh.dtype)
            return 0

        lax.fori_loop(0, heads, clear, 0)

    @pl.when(jnp.logical_not(has_down))
    def _():
        def clear(h, _):
            kvh[1, h] = jnp.zeros(kvh.shape[2:], kvh.dtype)
            return 0

        lax.fori_loop(0, heads, clear, 0)

    def own_send(i):
        return remote(qo.at[i // 2, i % 2], rq.at[i, 0:2], m_sent.at[0], m_sem.at[0, i], back)

    def relay_one(i):
        return remote(rq.at[i, 0:2], rq.at[i, 2:4], m_sent.at[1], m_sem.at[1, i], back)

    def relay_two(i):
        return remote(rq.at[i, 2], rq.at[i, 4], m_sent.at[2], m_sem.at[2, i], back)

    def halo_to(direction, h, device):
        return remote(
            kvo.at[h], kvh.at[direction, h], halo_sent.at[direction], halo_sem.at[direction, h], device
        )

    slots = ((3, 5), (1, 3), (0, 1))

    def out_send(which, i):
        lo, hi = slots[which]
        return (
            remote(so.at[i, lo:hi], ro.at[i, lo:hi], n_sent.at[which], n_sem.at[which, i], ahead),
            remote(sl.at[i, lo:hi], rl.at[i, lo:hi], l_sent.at[which], l_sem.at[which, i], ahead),
        )

    def far(i, which, joined):
        lo, hi = slots[which]
        h = i // 2
        width = (hi - lo) * HD
        queries = rq[i, lo:hi].reshape(width, HD)
        seen = []
        for side in (2, 1):
            flags = [rm[j, j + side : j + side + 1, :] > 0.5 for j in range(lo, hi)]
            seen.append(jnp.concatenate([jnp.where(f, 1.0, 0.0) for f in flags], axis=1) > 0.5)
        parts = []
        for x in range(2):
            scores = scores_of(kvo[h, 0, x], queries)
            parts.append((scores, vt[h, x], [(0, scores.shape[0], seen[x])]))
        out, total, top = attend(parts)
        lse, scale = settle(total, top)
        if joined is not None:
            joined()
        for n, j in enumerate(range(lo, hi)):
            lanes = slice(n * HD, (n + 1) * HD)
            part, own_lse, own_scale = out[:, lanes], lse[:, lanes], scale[:, lanes]
            if joined is not None:
                wa, wb, new_lse = merge(own_lse, rl[i, j + 2])
                part = part * (own_scale * wa) + ro[i, j + 2].astype(jnp.float32) * wb
                own_lse = new_lse
            else:
                part = part * own_scale
            so[i, j] = part.astype(jnp.bfloat16)
            sl[i, j] = own_lse
        for copy in out_send(which, i):
            copy.start()

    def own(i):
        h, f = i // 2, i % 2
        second = jnp.full((1, HD), f, jnp.int32) > 0
        first = jnp.full((1, HD), f, jnp.int32) >= 0
        for x in range(2):
            queries = qo[h, f, x]
            reach_up, reach_down = om[x, 0:1, :], om[x, 7:8, :]
            parts = [
                (scores_of(kvo[h, 0, x], queries), vt[h, x], [(0, 128, first), (128, 128, second)])
            ]
            for direction, reach in ((0, reach_up), (1, reach_down)):
                groups = []
                for frame in range(2):
                    for row in range(2):
                        need = 2 - row if direction == 0 else 1 + row
                        seen = reach > need - 0.5
                        if frame:
                            seen = seen & second
                        groups.append((frame * 128 + row * 64, 64, seen))
                parts.append(
                    (scores_of(kvh[direction, h, 0, x], queries), vth[direction, x], groups)
                )
            if x == 1:
                parts.append(
                    (scores_of(kvo[h, 0, 0], queries), vt[h, 0], [(0, 256, om[1, 1:2, :] > 0.5)])
                )
            out, total, top = attend(parts)
            lse, scale = settle(total, top)
            wa, wb, _ = merge(lse, rl[i, x])
            whole = out * (scale * wa) + ro[i, x].astype(jnp.float32) * wb
            outs[h, f, x] = whole.T.astype(jnp.bfloat16)
        pltpu.make_async_copy(
            outs.at[h, f, core], out_ref.at[f, :, column(core, h)], out_sem.at[0]
        ).start()
        remote(
            outs.at[h, f, other],
            out_ref.at[f, :, column(core, h)],
            out_sem.at[1],
            out_sem.at[2],
            partner,
        ).start()

    def during(t, lag):
        i = t - lag
        return i, (i >= 0) & (i < chunks)

    def step(t, _):
        i2, live2 = during(t, LAGS[1])

        @pl.when(live2)
        def _():
            relay_one(i2).wait_recv()

            @pl.when(i2 == 0)
            def _():
                remote(rm.at[0:2], rm.at[2:4], x_sent.at[4], meta_sem.at[3], back).wait_recv()
                remote(rm.at[2], rm.at[4], x_sent.at[5], meta_sem.at[4], back).start()

            relay_two(i2).start()

        i1, live1 = during(t, LAGS[0])

        @pl.when(live1)
        def _():
            own_send(i1).wait_recv()

            @pl.when(i1 == 0)
            def _():
                remote(om, rm.at[0:2], x_sent.at[3], meta_sem.at[2], back).wait_recv()
                remote(rm.at[0:2], rm.at[2:4], x_sent.at[4], meta_sem.at[3], back).start()

            relay_one(i1).start()

        @pl.when(t < chunks)
        def _():
            h = t // 2

            @pl.when(t % 2 == 0)
            def _():
                arrived(qo.at[h, :, core], q_local.at[h])
                arrived(qo.at[h, :, other], q_remote.at[h])

            @pl.when(t == 0)
            def _():
                arrived(om.at[core], meta_sem.at[0])
                arrived(om.at[other], meta_sem.at[1])
                remote(om, rm.at[0:2], x_sent.at[3], meta_sem.at[2], back).start()

            own_send(t).start()

            @pl.when(t == 0)
            def _():
                arrived(kvo.at[:, :, core], kv_sem.at[0])
                arrived(kvo.at[:, :, other], kv_sem.at[1])

            @pl.when(t % 2 == 0)
            def _():
                @pl.when(has_down)
                def _():
                    halo_to(0, h, down).start()

                @pl.when(has_up)
                def _():
                    halo_to(1, h, up).start()

        i3, live3 = during(t, LAGS[2])

        @pl.when(live3)
        def _():
            @pl.when(i3 % 2 == 0)
            def _():
                for x in range(2):
                    vt[i3 // 2, x] = kvo[i3 // 2, 1, x].T

            relay_two(i3).wait_recv()

            @pl.when(i3 == 0)
            def _():
                remote(rm.at[2], rm.at[4], x_sent.at[5], meta_sem.at[4], back).wait_recv()

            far(i3, 0, None)

        for which in (1, 2):
            i, live = during(t, LAGS[2 + which])

            @pl.when(live)
            def _():
                def joined():
                    for copy in out_send(which - 1, i):
                        copy.wait_recv()

                far(i, which, joined)

        i6, live6 = during(t, LAGS[5])

        @pl.when(live6)
        def _():
            h = i6 // 2

            @pl.when(i6 % 2 == 0)
            def _():
                @pl.when(has_up)
                def _():
                    halo_to(0, h, down).wait_recv()

                @pl.when(has_down)
                def _():
                    halo_to(1, h, up).wait_recv()

                for direction in range(2):
                    for x in range(2):
                        vth[direction, x] = kvh[direction, h, 1, x].T

            for copy in out_send(2, i6):
                copy.wait_recv()
            own(i6)

        return 0

    lax.fori_loop(0, chunks + LAGS[5], step, 0)

    arrived(meta_ref, x_sent.at[0])
    arrived(qo.at[:, :, core], x_sent.at[1])
    arrived(kvo.at[:, :, core], x_sent.at[2])
    arrived(om, x_sent.at[3])
    arrived(rm.at[0:2], x_sent.at[4])
    arrived(rm.at[2], x_sent.at[5])
    arrived(qo, m_sent.at[0])
    arrived(rq.at[:, 0:2], m_sent.at[1])
    arrived(rq.at[:, 2], m_sent.at[2])
    for which, (lo, hi) in enumerate(slots):
        arrived(so.at[:, lo:hi], n_sent.at[which])
        arrived(sl.at[:, lo:hi], l_sent.at[which])

    @pl.when(has_down)
    def _():
        arrived(kvo, halo_sent.at[0])

    @pl.when(has_up)
    def _():
        arrived(kvo, halo_sent.at[1])

    for i in range(3):
        arrived(outs.at[:, :, 0], out_sem.at[i])


def local(blocks, tiles, queries, keys, values, neighbours, halo_rows):
    frames, rows, width, channels = queries.shape
    tokens = frames * rows * width
    heads = channels // HD // 2
    chunks = 2 * heads
    block = lax.axis_index("tm")
    tile = lax.axis_index("tile")
    listed = neighbours[0, 0]
    distance = jnp.arange(8, dtype=jnp.int32)
    hit = (listed[None, :] >= 0) & (listed[None, :] == block - distance[:, None])
    hit = jnp.any(hit, axis=1) & (distance >= 1) & (distance <= WIN)
    reach = halo_rows[0, 0]
    meta = jnp.where(hit, 1, 0)
    meta = jnp.where(distance == 0, jnp.where(tile > 0, reach, 0), meta)
    meta = jnp.where(distance == 7, jnp.where(tile < tiles - 1, reach, 0), meta)
    meta = jnp.broadcast_to(meta.astype(jnp.float32)[:, None], (8, HD))
    half = tokens // 2
    bf16, f32 = jnp.bfloat16, jnp.float32
    dma = pltpu.SemaphoreType.DMA
    result = pl.pallas_call(
        functools.partial(kernel, blocks, tiles, heads),
        out_shape=jax.ShapeDtypeStruct((2, half, channels), bf16),
        in_specs=[pl.BlockSpec(memory_space=pl.ANY)] * 3 + [pl.BlockSpec(memory_space=pltpu.VMEM)],
        out_specs=pl.BlockSpec(memory_space=pl.ANY),
        scratch_shapes=[
            pltpu.VMEM((heads, 2, 2, half, HD), bf16),
            pltpu.VMEM((heads, 2, 2, tokens, HD), bf16),
            pltpu.VMEM((2, heads, 2, 2, tokens, HD), bf16),
            pltpu.VMEM((heads, 2, HD, tokens), bf16),
            pltpu.VMEM((2, 2, HD, tokens), bf16),
            pltpu.VMEM((chunks, 5, half, HD), bf16),
            pltpu.VMEM((chunks, 5, HD, half), bf16),
            pltpu.VMEM((chunks, 5, 1, half), f32),
            pltpu.VMEM((chunks, 5, HD, half), bf16),
            pltpu.VMEM((chunks, 5, 1, half), f32),
            pltpu.VMEM((heads, 2, 2, half, HD), bf16),
            pltpu.VMEM((2, 8, HD), f32),
            pltpu.VMEM((5, 8, HD), f32),
            dma((heads,)),
            dma((heads,)),
            dma((2,)),
            dma((5,)),
            dma((2, heads)),
            dma((3, chunks)),
            dma((3, chunks)),
            dma((3, chunks)),
            dma((3,)),
            dma((3,)),
            dma((3,)),
            dma((6,)),
            dma((2,)),
            dma((3,)),
        ],
        compiler_params=pltpu.CompilerParams(
            collective_id=0, has_side_effects=True, vmem_limit_bytes=48 * 1024 * 1024
        ),
    )(
        queries.reshape(2, half, channels),
        keys.reshape(tokens, channels),
        values.reshape(tokens, channels),
        meta,
    )
    return result.reshape(frames, rows, width, channels)


def solution(mesh):
    body = functools.partial(local, mesh.shape["tm"], mesh.shape["tile"])
    return jax.shard_map(
        body,
        mesh=mesh,
        in_specs=(
            P("tm", "tile", None, None),
            P("tm", "tile", None, None),
            P("tm", "tile", None, None),
            P("tm", "tile", None),
            P("tm", "tile"),
        ),
        out_specs=P("tm", "tile", None, None),
        check_vma=False,
    )
```

time: 418 us -> 157 us (0.38)
  the two profiles are of different devices: /device:TPU:56 before, /device:TPU:7 now
where the time goes in v1:
time: 157 us
  Pallas kernels  150 us (96%)
  local copies, waits for them, and re-layouts  5.08 us (3%)
    pallas_call x1, Pallas kernels, local(): pl.pallas_call(functools.partial(kernel, blocks, tiles, heads), out_shape...  150 us
    unnamed x7, local copies, waits for them, and re-layouts  5.01 us

profile of v1, /device:TPU:7, one launch (start us, length us, event | category | flops | bytes accessed | tf_op | source)
XLA Modules:
  0.0 156.9 jit_solution(14748280190869005674)
XLA Ops:
  0.7 0.7 broadcast_compare_fusion
  1.3 0.7 and_reduce_fusion
  2.1 0.1 broadcast_in_dim.21.meta_ref
  2.2 0.0 copy-start
  2.2 1.3 copy-done
  3.5 0.0 copy-start.1
  3.5 1.3 copy-done.1
  4.8 0.0 copy-start.2
  4.8 1.3 copy-done.2
  6.1 149.8 %shard_map.55 = bf16[2,128,2560]{2,1,0:T(8,128)(2,1)S(1)} custom-call(bf16[2,128,2560]{2,1,0:T(8,128)(2,1)S(1)} %bitcast.10, bf16[256,2560]{1,0:T(8,128)(2,1)S(1)} %bitcast.11, bf16[256,2560]{1,0:T(8,128)(2,1)S(1)} %bitcast.12, f32[8,128]{1,0:T(8,128)S(1)} %broadcast_in_dim.21.meta_ref), custom_call_target="tpu_custom_call" | custom-call | tf_op jit(solution)/shard_map/pallas_call | solution.py:444
  155.9 1.1 copy.8
  (2 shorter events, 0.0 us)
Async XLA Ops:
  2.2 1.3 copy-start
  3.5 1.3 copy-start.1
  4.8 1.3 copy-start.2

commit v2 on v1

--- a/solution.py
+++ b/solution.py
@@ -9,10 +9,10 @@
 from jax.sharding import PartitionSpec as P
 
 HD = 128
-WIN = 5
 BIG = 1e30
 SCALE = math.log2(math.e) / math.sqrt(HD)
-LAGS = (1, 2, 3, 4, 5, 6)
+LAGS = (2, 4, 6, 8, 10, 12)
+RELAY = 5
 MESH = pl.DeviceIdType.MESH
 
 
@@ -64,7 +64,8 @@
     q_ref,
     k_ref,
     v_ref,
-    meta_ref,
+    list_ref,
+    reach_ref,
     out_ref,
     qo,
     kvo,
@@ -102,10 +103,20 @@
     partner = {"tm": me + 1 - 2 * core}
     back = {"tm": lax.rem(me + blocks - 2, blocks)}
     ahead = {"tm": lax.rem(me + 2, blocks)}
-    up = {"tile": lax.max(tile - 1, 0)}
-    down = {"tile": lax.min(tile + 1, tiles - 1)}
+    across = lax.rem(me + blocks // 2, blocks)
     has_up = tile > 0
     has_down = tile < tiles - 1
+    has_ahead = me < blocks - 2
+    has_back = me >= 2
+    upper, lower, last = tiles // 2 - 1, tiles // 2, tiles - 1
+    chip = me // 2
+    chips = blocks // 2
+    at_end = (chip == 0) | (chip == chips - 1)
+    at_edge = at_end | (chip == chips // 2 - 1) | (chip == chips // 2)
+    detours = at_edge & ((tile == upper) | (tile == lower))
+    relays = at_edge & ((tile == 0) | (tile == last))
+    takes_up = has_up | (relays & (tile == 0))
+    takes_down = has_down | (relays & (tile == last))
 
     def remote(src, dst, sent, received, device):
         return pltpu.make_async_remote_copy(
@@ -128,7 +139,19 @@
     for device in (partner, back, ahead) + rings:
         pl.semaphore_signal(barrier, inc=1, device_id=device, device_id_type=MESH)
 
-    pltpu.make_async_copy(meta_ref, om.at[core], meta_sem.at[0]).start()
+    @pl.when(detours)
+    def _():
+        for n in (0, tiles - 1):
+            pl.semaphore_signal(
+                barrier, inc=1, device_id={"tm": across, "tile": n}, device_id_type=MESH
+            )
+
+    @pl.when(relays)
+    def _():
+        for n in (upper, lower):
+            pl.semaphore_signal(
+                barrier, inc=1, device_id={"tm": across, "tile": n}, device_id_type=MESH
+            )
 
     def fetch_q(h, _):
         pltpu.make_async_copy(
@@ -146,9 +169,44 @@
     lax.fori_loop(0, heads, fetch_q, 0)
     lax.fori_loop(0, heads, fetch_kv, 0)
 
-    pl.semaphore_wait(barrier, 5)
-
-    remote(meta_ref, om.at[core], x_sent.at[0], meta_sem.at[1], partner).start()
+    distance = lax.broadcasted_iota(jnp.int32, (8, HD), 0)
+    meta = jnp.zeros((8, HD), jnp.float32)
+    for n in range(list_ref.shape[0]):
+        block = list_ref[n]
+        meta = jnp.where(distance == jnp.where(block >= 0, me - block, 0), 1.0, meta)
+    reach = reach_ref[0].astype(jnp.float32)
+    meta = jnp.where(distance == 0, jnp.where(has_up, reach, 0.0), meta)
+    meta = jnp.where(distance == 7, jnp.where(has_down, reach, 0.0), meta)
+    om[core] = meta
+
+    @pl.when(jnp.logical_not(has_ahead))
+    def _():
+        rm[...] = jnp.zeros(rm.shape, rm.dtype)
+
+        def clear(i, _):
+            rq[i] = jnp.zeros(rq.shape[1:], rq.dtype)
+            return 0
+
+        lax.fori_loop(0, chunks, clear, 0)
+
+    @pl.when(jnp.logical_not(has_back))
+    def _():
+        def clear(i, _):
+            ro[i] = jnp.zeros(ro.shape[1:], ro.dtype)
+            rl[i] = jnp.full(rl.shape[1:], -BIG, rl.dtype)
+            return 0
+
+        lax.fori_loop(0, chunks, clear, 0)
+
+    @pl.when(detours | relays)
+    def _():
+        pl.semaphore_wait(barrier, 7)
+
+    @pl.when(jnp.logical_not(detours | relays))
+    def _():
+        pl.semaphore_wait(barrier, 5)
+
+    remote(om.at[core], om.at[core], x_sent.at[0], meta_sem.at[0], partner).start()
 
     def give_q(h, _):
         remote(
@@ -166,7 +224,7 @@
     lax.fori_loop(0, heads, give_q, 0)
     lax.fori_loop(0, heads, give_kv, 0)
 
-    @pl.when(jnp.logical_not(has_up))
+    @pl.when(jnp.logical_not(takes_up))
     def _():
         def clear(h, _):
             kvh[0, h] = jnp.zeros(kvh.shape[2:], kvh.dtype)
@@ -174,7 +232,7 @@
 
         lax.fori_loop(0, heads, clear, 0)
 
-    @pl.when(jnp.logical_not(has_down))
+    @pl.when(jnp.logical_not(takes_down))
     def _():
         def clear(h, _):
             kvh[1, h] = jnp.zeros(kvh.shape[2:], kvh.dtype)
@@ -191,10 +249,62 @@
     def relay_two(i):
         return remote(rq.at[i, 2], rq.at[i, 4], m_sent.at[2], m_sem.at[2, i], back)
 
-    def halo_to(direction, h, device):
+    def halo(direction, h, device, src=None):
         return remote(
-            kvo.at[h], kvh.at[direction, h], halo_sent.at[direction], halo_sem.at[direction, h], device
+            kvo.at[h] if src is None else src,
+            kvh.at[direction, h],
+            halo_sent.at[0 if src is None else 1],
+            halo_sem.at[direction, h],
+            device,
         )
+
+    down = {"tm": me, "tile": tile + 1}
+    up = {"tm": me, "tile": tile - 1}
+
+    def opposite(n):
+        return {"tm": across, "tile": n}
+
+    def halo_out(h):
+        @pl.when(has_down & jnp.logical_not(detours & (tile == upper)))
+        def _():
+            halo(0, h, down).start()
+
+        @pl.when(has_up & jnp.logical_not(detours & (tile == lower)))
+        def _():
+            halo(1, h, up).start()
+
+        by_last = (at_end & (tile == upper)) | (jnp.logical_not(at_end) & (tile == lower))
+
+        @pl.when(detours & by_last)
+        def _():
+            halo(1, h, opposite(last)).start()
+
+        @pl.when(detours & jnp.logical_not(by_last))
+        def _():
+            halo(0, h, opposite(0)).start()
+
+    def halo_relay(h):
+        for held, edge in ((0, 0), (1, last)):
+
+            @pl.when(relays & (tile == edge))
+            def _():
+                halo(held, h, partner).wait_recv()
+
+            for end in (True, False):
+                onto = held if end else 1 - held
+
+                @pl.when(relays & (tile == edge) & (at_end if end else jnp.logical_not(at_end)))
+                def _():
+                    halo(onto, h, opposite(upper if onto else lower), kvh.at[held, h]).start()
+
+    def halo_in(h):
+        @pl.when(has_up)
+        def _():
+            halo(0, h, partner).wait_recv()
+
+        @pl.when(has_down)
+        def _():
+            halo(1, h, partner).wait_recv()
 
     slots = ((3, 5), (1, 3), (0, 1))
 
@@ -205,7 +315,13 @@
             remote(sl.at[i, lo:hi], rl.at[i, lo:hi], l_sent.at[which], l_sem.at[which, i], ahead),
         )
 
-    def far(i, which, joined):
+    def join(which, i):
+        @pl.when(has_back)
+        def _():
+            for copy in out_send(which, i):
+                copy.wait_recv()
+
+    def far(i, which):
         lo, hi = slots[which]
         h = i // 2
         width = (hi - lo) * HD
@@ -220,12 +336,12 @@
             parts.append((scores, vt[h, x], [(0, scores.shape[0], seen[x])]))
         out, total, top = attend(parts)
         lse, scale = settle(total, top)
-        if joined is not None:
-            joined()
+        if which:
+            join(which - 1, i)
         for n, j in enumerate(range(lo, hi)):
             lanes = slice(n * HD, (n + 1) * HD)
             part, own_lse, own_scale = out[:, lanes], lse[:, lanes], scale[:, lanes]
-            if joined is not None:
+            if which:
                 wa, wb, new_lse = merge(own_lse, rl[i, j + 2])
                 part = part * (own_scale * wa) + ro[i, j + 2].astype(jnp.float32) * wb
                 own_lse = new_lse
@@ -233,8 +349,10 @@
                 part = part * own_scale
             so[i, j] = part.astype(jnp.bfloat16)
             sl[i, j] = own_lse
-        for copy in out_send(which, i):
-            copy.start()
+        @pl.when(has_ahead)
+        def _():
+            for copy in out_send(which, i):
+                copy.start()
 
     def own(i):
         h, f = i // 2, i % 2
@@ -264,6 +382,8 @@
                 )
             out, total, top = attend(parts)
             lse, scale = settle(total, top)
+            if x == 0:
+                join(2, i)
             wa, wb, _ = merge(lse, rl[i, x])
             whole = out * (scale * wa) + ro[i, x].astype(jnp.float32) * wb
             outs[h, f, x] = whole.T.astype(jnp.bfloat16)
@@ -282,64 +402,60 @@
         i = t - lag
         return i, (i >= 0) & (i < chunks)
 
+    def meta_send(n):
+        src, dst = ((om, rm.at[0:2]), (rm.at[0:2], rm.at[2:4]), (rm.at[2], rm.at[4]))[n]
+        return remote(src, dst, x_sent.at[3 + n], meta_sem.at[1 + n], back)
+
+    sends = (own_send, relay_one, relay_two)
+
+    def pass_back(t, n):
+        i, live = (t, t < chunks) if n == 0 else during(t, LAGS[n - 1])
+
+        if n:
+
+            @pl.when(live & has_ahead)
+            def _():
+                sends[n - 1](i).wait_recv()
+
+                @pl.when(i == 0)
+                def _():
+                    meta_send(n - 1).wait_recv()
+
+        @pl.when(live & has_back)
+        def _():
+            @pl.when(i == 0)
+            def _():
+                meta_send(n).start()
+
+            sends[n](i).start()
+
     def step(t, _):
-        i2, live2 = during(t, LAGS[1])
-
-        @pl.when(live2)
-        def _():
-            relay_one(i2).wait_recv()
-
-            @pl.when(i2 == 0)
-            def _():
-                remote(rm.at[0:2], rm.at[2:4], x_sent.at[4], meta_sem.at[3], back).wait_recv()
-                remote(rm.at[2], rm.at[4], x_sent.at[5], meta_sem.at[4], back).start()
-
-            relay_two(i2).start()
-
-        i1, live1 = during(t, LAGS[0])
-
-        @pl.when(live1)
-        def _():
-            own_send(i1).wait_recv()
-
-            @pl.when(i1 == 0)
-            def _():
-                remote(om, rm.at[0:2], x_sent.at[3], meta_sem.at[2], back).wait_recv()
-                remote(rm.at[0:2], rm.at[2:4], x_sent.at[4], meta_sem.at[3], back).start()
-
-            relay_one(i1).start()
-
-        @pl.when(t < chunks)
-        def _():
-            h = t // 2
-
-            @pl.when(t % 2 == 0)
-            def _():
-                arrived(qo.at[h, :, core], q_local.at[h])
-                arrived(qo.at[h, :, other], q_remote.at[h])
-
-            @pl.when(t == 0)
-            def _():
-                arrived(om.at[core], meta_sem.at[0])
-                arrived(om.at[other], meta_sem.at[1])
-                remote(om, rm.at[0:2], x_sent.at[3], meta_sem.at[2], back).start()
-
-            own_send(t).start()
-
-            @pl.when(t == 0)
-            def _():
-                arrived(kvo.at[:, :, core], kv_sem.at[0])
-                arrived(kvo.at[:, :, other], kv_sem.at[1])
-
-            @pl.when(t % 2 == 0)
-            def _():
-                @pl.when(has_down)
-                def _():
-                    halo_to(0, h, down).start()
-
-                @pl.when(has_up)
-                def _():
-                    halo_to(1, h, up).start()
+        @pl.when((t < chunks) & (t % 2 == 0))
+        def _():
+            arrived(qo.at[t // 2, :, core], q_local.at[t // 2])
+            arrived(qo.at[t // 2, :, other], q_remote.at[t // 2])
+
+        @pl.when(t == 0)
+        def _():
+            arrived(om.at[other], meta_sem.at[0])
+
+        for n in (2, 1, 0):
+            pass_back(t, n)
+
+        @pl.when(t == 0)
+        def _():
+            arrived(kvo.at[:, :, core], kv_sem.at[0])
+            arrived(kvo.at[:, :, other], kv_sem.at[1])
+
+        @pl.when((t < chunks) & (t % 2 == 0))
+        def _():
+            halo_out(t // 2)
+
+        ih, liveh = during(t, RELAY)
+
+        @pl.when(liveh & (ih % 2 == 0))
+        def _():
+            halo_relay(ih // 2)
 
         i3, live3 = during(t, LAGS[2])
 
@@ -350,24 +466,22 @@
                 for x in range(2):
                     vt[i3 // 2, x] = kvo[i3 // 2, 1, x].T
 
-            relay_two(i3).wait_recv()
-
-            @pl.when(i3 == 0)
+            @pl.when(has_ahead)
             def _():
-                remote(rm.at[2], rm.at[4], x_sent.at[5], meta_sem.at[4], back).wait_recv()
-
-            far(i3, 0, None)
+                relay_two(i3).wait_recv()
+
+                @pl.when(i3 == 0)
+                def _():
+                    meta_send(2).wait_recv()
+
+            far(i3, 0)
 
         for which in (1, 2):
             i, live = during(t, LAGS[2 + which])
 
             @pl.when(live)
             def _():
-                def joined():
-                    for copy in out_send(which - 1, i):
-                        copy.wait_recv()
-
-                far(i, which, joined)
+                far(i, which)
 
         i6, live6 = during(t, LAGS[5])
 
@@ -377,44 +491,45 @@
 
             @pl.when(i6 % 2 == 0)
             def _():
-                @pl.when(has_up)
-                def _():
-                    halo_to(0, h, down).wait_recv()
-
-                @pl.when(has_down)
-                def _():
-                    halo_to(1, h, up).wait_recv()
-
+                halo_in(h)
                 for direction in range(2):
                     for x in range(2):
                         vth[direction, x] = kvh[direction, h, 1, x].T
 
-            for copy in out_send(2, i6):
-                copy.wait_recv()
             own(i6)
 
         return 0
 
     lax.fori_loop(0, chunks + LAGS[5], step, 0)
 
-    arrived(meta_ref, x_sent.at[0])
+    arrived(om.at[core], x_sent.at[0])
     arrived(qo.at[:, :, core], x_sent.at[1])
     arrived(kvo.at[:, :, core], x_sent.at[2])
-    arrived(om, x_sent.at[3])
-    arrived(rm.at[0:2], x_sent.at[4])
-    arrived(rm.at[2], x_sent.at[5])
-    arrived(qo, m_sent.at[0])
-    arrived(rq.at[:, 0:2], m_sent.at[1])
-    arrived(rq.at[:, 2], m_sent.at[2])
-    for which, (lo, hi) in enumerate(slots):
-        arrived(so.at[:, lo:hi], n_sent.at[which])
-        arrived(sl.at[:, lo:hi], l_sent.at[which])
-
-    @pl.when(has_down)
+
+    @pl.when(has_back)
+    def _():
+        arrived(om, x_sent.at[3])
+        arrived(rm.at[0:2], x_sent.at[4])
+        arrived(rm.at[2], x_sent.at[5])
+        arrived(qo, m_sent.at[0])
+        arrived(rq.at[:, 0:2], m_sent.at[1])
+        arrived(rq.at[:, 2], m_sent.at[2])
+
+    @pl.when(has_ahead)
+    def _():
+        for which, (lo, hi) in enumerate(slots):
+            arrived(so.at[:, lo:hi], n_sent.at[which])
+            arrived(sl.at[:, lo:hi], l_sent.at[which])
+
+    @pl.when(has_down & has_up)
+    def _():
+        arrived(kvh, halo_sent.at[0])
+
+    @pl.when(jnp.logical_not(has_down & has_up))
     def _():
         arrived(kvo, halo_sent.at[0])
 
-    @pl.when(has_up)
+    @pl.when(relays)
     def _():
         arrived(kvo, halo_sent.at[1])
 
@@ -427,24 +542,14 @@
     tokens = frames * rows * width
     heads = channels // HD // 2
     chunks = 2 * heads
-    block = lax.axis_index("tm")
-    tile = lax.axis_index("tile")
-    listed = neighbours[0, 0]
-    distance = jnp.arange(8, dtype=jnp.int32)
-    hit = (listed[None, :] >= 0) & (listed[None, :] == block - distance[:, None])
-    hit = jnp.any(hit, axis=1) & (distance >= 1) & (distance <= WIN)
-    reach = halo_rows[0, 0]
-    meta = jnp.where(hit, 1, 0)
-    meta = jnp.where(distance == 0, jnp.where(tile > 0, reach, 0), meta)
-    meta = jnp.where(distance == 7, jnp.where(tile < tiles - 1, reach, 0), meta)
-    meta = jnp.broadcast_to(meta.astype(jnp.float32)[:, None], (8, HD))
     half = tokens // 2
     bf16, f32 = jnp.bfloat16, jnp.float32
     dma = pltpu.SemaphoreType.DMA
     result = pl.pallas_call(
         functools.partial(kernel, blocks, tiles, heads),
         out_shape=jax.ShapeDtypeStruct((2, half, channels), bf16),
-        in_specs=[pl.BlockSpec(memory_space=pl.ANY)] * 3 + [pl.BlockSpec(memory_space=pltpu.VMEM)],
+        in_specs=[pl.BlockSpec(memory_space=pl.ANY)] * 3
+        + [pl.BlockSpec(memory_space=pltpu.SMEM)] * 2,
         out_specs=pl.BlockSpec(memory_space=pl.ANY),
         scratch_shapes=[
             pltpu.VMEM((heads, 2, 2, half, HD), bf16),
@@ -463,7 +568,7 @@
             dma((heads,)),
             dma((heads,)),
             dma((2,)),
-            dma((5,)),
+            dma((4,)),
             dma((2, heads)),
             dma((3, chunks)),
             dma((3, chunks)),
@@ -476,13 +581,14 @@
             dma((3,)),
         ],
         compiler_params=pltpu.CompilerParams(
-            collective_id=0, has_side_effects=True, vmem_limit_bytes=48 * 1024 * 1024
+            collective_id=0, has_side_effects=True, vmem_limit_bytes=62 * 1024 * 1024
         ),
     )(
         queries.reshape(2, half, channels),
         keys.reshape(tokens, channels),
         values.reshape(tokens, channels),
-        meta,
+        neighbours.reshape(-1),
+        halo_rows.reshape(-1),
     )
     return result.reshape(frames, rows, width, channels)
 

time: 157 us -> 116 us (0.74); the launches traced: 157 us -> 114 us
  Pallas kernels: 150 us -> 111 us
  local copies, waits for them, and re-layouts: 5.08 us -> 2.46 us
    pallas_call x1, Pallas kernels: 150 us -> 111 us  [local(): pl.pallas_call(functools.partial(kernel, blocks, tiles, heads), out_shape...]
    unnamed x7 -> x1, local copies, waits for them, and re-layouts: 5.01 us -> 2.46 us
where the time goes in v2:
time: 116 us; the launch traced here: 114 us
  Pallas kernels  111 us (96%)
  local copies, waits for them, and re-layouts  2.46 us (2%)
    pallas_call x1, Pallas kernels, local(): pl.pallas_call(functools.partial(kernel, blocks, tiles, heads), out_shape...  111 us
    unnamed x1, local copies, waits for them, and re-layouts  2.46 us

profile of v2, /device:TPU:7, one launch (start us, length us, event | category | flops | bytes accessed | tf_op | source)
XLA Modules:
  0.0 114.3 jit_solution(5357146495110799464)
XLA Ops:
  0.7 111.2 %shard_map.55 = bf16[2,128,2560]{2,1,0:T(8,128)(2,1)} custom-call(bf16[2,128,2560]{2,1,0:T(8,128)(2,1)} %bitcast.8, bf16[256,2560]{1,0:T(8,128)(2,1)} %bitcast.9, bf16[256,2560]{1,0:T(8,128)(2,1)} %bitcast.10, s32[3]{0:T(128)} %bitcast.11, s32[1]{0:T(128)} %bitcast.6.reach_ref), custom_call_target="tpu_custom_call" | custom-call | tf_op jit(solution)/shard_map/pallas_call | solution.py:548
  111.8 2.5 %copy.8 = bf16[2,2,64,2560]{3,2,1,0:T(8,128)(2,1)} copy(bf16[2,2,64,2560]{3,2,1,0:T(8,128)(2,1)} %bitcast.7) | data formatting | bytes 2621440

commit v3 on v2

--- a/solution.py
+++ b/solution.py
@@ -11,8 +11,10 @@
 HD = 128
 BIG = 1e30
 SCALE = math.log2(math.e) / math.sqrt(HD)
-LAGS = (2, 4, 6, 8, 10, 12)
-RELAY = 5
+AHEAD = 2
+KV_STEP = 7
+LAGS = (0, 2, 3, 5, 7, 9)
+RELAY = 4
 MESH = pl.DeviceIdType.MESH
 
 
@@ -80,6 +82,7 @@
     outs,
     om,
     rm,
+    rk,
     q_local,
     q_remote,
     kv_sem,
@@ -93,9 +96,12 @@
     l_sent,
     x_sent,
     halo_sent,
+    k_sem,
+    k_sent,
     out_sem,
 ):
-    chunks = 2 * heads
+    kv_head = heads - 1
+    chunks = 2 * kv_head
     me = lax.axis_index("tm")
     tile = lax.axis_index("tile")
     core = lax.rem(me, 2)
@@ -197,6 +203,9 @@
             return 0
 
         lax.fori_loop(0, chunks, clear, 0)
+        for n in range(rk.shape[0]):
+            for i in range(2):
+                rk[n, i] = jnp.zeros(rk.shape[2:], rk.dtype)
 
     @pl.when(detours | relays)
     def _():
@@ -222,7 +231,32 @@
         return 0
 
     lax.fori_loop(0, heads, give_q, 0)
+
+    def own_send(i):
+        return remote(qo.at[i // 2, i % 2], rq.at[i, 0:2], m_sent.at[0], m_sem.at[0, i], back)
+
+    def meta_send(n):
+        src, dst = ((om, rm.at[0:2]), (rm.at[0:2], rm.at[2:4]), (rm.at[2], rm.at[4]))[n]
+        return remote(src, dst, x_sent.at[3 + n], meta_sem.at[1 + n], back)
+
+    def await_queries(h):
+        arrived(qo.at[h, :, core], q_local.at[h])
+        arrived(qo.at[h, :, other], q_remote.at[h])
+
+    for i in range(AHEAD):
+        if i % 2 == 0:
+            await_queries(i // 2)
+
+        @pl.when(has_back)
+        def _():
+            own_send(i).start()
+
     lax.fori_loop(0, heads, give_kv, 0)
+    arrived(om.at[other], meta_sem.at[0])
+
+    @pl.when(has_back)
+    def _():
+        meta_send(0).start()
 
     @pl.when(jnp.logical_not(takes_up))
     def _():
@@ -239,9 +273,6 @@
             return 0
 
         lax.fori_loop(0, heads, clear, 0)
-
-    def own_send(i):
-        return remote(qo.at[i // 2, i % 2], rq.at[i, 0:2], m_sent.at[0], m_sem.at[0, i], back)
 
     def relay_one(i):
         return remote(rq.at[i, 0:2], rq.at[i, 2:4], m_sent.at[1], m_sem.at[1, i], back)
@@ -354,39 +385,31 @@
             for copy in out_send(which, i):
                 copy.start()
 
-    def own(i):
-        h, f = i // 2, i % 2
+    def near(h, f, x):
+        queries = qo[h, f, x]
         second = jnp.full((1, HD), f, jnp.int32) > 0
         first = jnp.full((1, HD), f, jnp.int32) >= 0
-        for x in range(2):
-            queries = qo[h, f, x]
-            reach_up, reach_down = om[x, 0:1, :], om[x, 7:8, :]
-            parts = [
-                (scores_of(kvo[h, 0, x], queries), vt[h, x], [(0, 128, first), (128, 128, second)])
-            ]
-            for direction, reach in ((0, reach_up), (1, reach_down)):
-                groups = []
-                for frame in range(2):
-                    for row in range(2):
-                        need = 2 - row if direction == 0 else 1 + row
-                        seen = reach > need - 0.5
-                        if frame:
-                            seen = seen & second
-                        groups.append((frame * 128 + row * 64, 64, seen))
-                parts.append(
-                    (scores_of(kvh[direction, h, 0, x], queries), vth[direction, x], groups)
-                )
-            if x == 1:
-                parts.append(
-                    (scores_of(kvo[h, 0, 0], queries), vt[h, 0], [(0, 256, om[1, 1:2, :] > 0.5)])
-                )
-            out, total, top = attend(parts)
-            lse, scale = settle(total, top)
-            if x == 0:
-                join(2, i)
-            wa, wb, _ = merge(lse, rl[i, x])
-            whole = out * (scale * wa) + ro[i, x].astype(jnp.float32) * wb
-            outs[h, f, x] = whole.T.astype(jnp.bfloat16)
+        half = kvo.shape[3] // 2
+        parts = [
+            (scores_of(kvo[h, 0, x], queries), vt[h, x], [(0, half, first), (half, half, second)])
+        ]
+        for direction, reach in ((0, om[x, 0:1, :]), (1, om[x, 7:8, :])):
+            groups = []
+            for frame in range(2):
+                for row in range(2):
+                    need = 2 - row if direction == 0 else 1 + row
+                    seen = reach > need - 0.5
+                    if frame:
+                        seen = seen & second
+                    groups.append((frame * half + row * half // 2, half // 2, seen))
+            parts.append((scores_of(kvh[direction, h, 0, x], queries), vth[direction, x], groups))
+        if x == 1:
+            parts.append(
+                (scores_of(kvo[h, 0, 0], queries), vt[h, 0], [(0, 2 * half, om[1, 1:2, :] > 0.5)])
+            )
+        return queries, parts
+
+    def give_out(h, f):
         pltpu.make_async_copy(
             outs.at[h, f, core], out_ref.at[f, :, column(core, h)], out_sem.at[0]
         ).start()
@@ -398,18 +421,67 @@
             partner,
         ).start()
 
+    def own(i):
+        h, f = i // 2, i % 2
+        for x in range(2):
+            _, parts = near(h, f, x)
+            out, total, top = attend(parts)
+            lse, scale = settle(total, top)
+            if x == 0:
+                join(2, i)
+            wa, wb, _ = merge(lse, rl[i, x])
+            whole = out * (scale * wa) + ro[i, x].astype(jnp.float32) * wb
+            outs[h, f, x] = whole.T.astype(jnp.bfloat16)
+        give_out(h, f)
+
+    def own_by_keys(f):
+        for x in range(2):
+            queries, parts = near(kv_head, f, x)
+            for distance in range(1 + x, 6):
+                n, side = divmod(distance - 1 - x, 2)
+                seen = om[x, distance : distance + 1, :] > 0.5
+                scores = scores_of(rk[n, 0, 1 - side], queries)
+                parts.append((scores, rk[n, 1, 1 - side].T, [(0, scores.shape[0], seen)]))
+            out, total, _ = attend(parts)
+            outs[kv_head, f, x] = (out * (1.0 / total)).T.astype(jnp.bfloat16)
+        give_out(kv_head, f)
+
+    def turn_values(h):
+        for x in range(2):
+            vt[h, x] = kvo[h, 1, x].T
+
+    def turn_halo(h):
+        for direction in range(2):
+            for x in range(2):
+                vth[direction, x] = kvh[direction, h, 1, x].T
+
     def during(t, lag):
         i = t - lag
         return i, (i >= 0) & (i < chunks)
 
-    def meta_send(n):
-        src, dst = ((om, rm.at[0:2]), (rm.at[0:2], rm.at[2:4]), (rm.at[2], rm.at[4]))[n]
-        return remote(src, dst, x_sent.at[3 + n], meta_sem.at[1 + n], back)
+    def key_send(n, i):
+        src, dst = (
+            (kvo.at[kv_head, i], rk.at[0, i]),
+            (rk.at[0, i], rk.at[1, i]),
+            (rk.at[1, i, 1], rk.at[2, i, 1]),
+        )[n]
+        return remote(src, dst, k_sent.at[n], k_sem.at[n, i], ahead)
+
+    def pass_ahead(n, i):
+        if n:
+
+            @pl.when(has_back)
+            def _():
+                key_send(n - 1, i).wait_recv()
+
+        @pl.when(has_ahead)
+        def _():
+            key_send(n, i).start()
 
     sends = (own_send, relay_one, relay_two)
 
     def pass_back(t, n):
-        i, live = (t, t < chunks) if n == 0 else during(t, LAGS[n - 1])
+        i, live = during(t, LAGS[n - 1] if n else -AHEAD)
 
         if n:
 
@@ -423,21 +495,18 @@
 
         @pl.when(live & has_back)
         def _():
-            @pl.when(i == 0)
-            def _():
-                meta_send(n).start()
+            if n:
+
+                @pl.when(i == 0)
+                def _():
+                    meta_send(n).start()
 
             sends[n](i).start()
 
     def step(t, _):
-        @pl.when((t < chunks) & (t % 2 == 0))
-        def _():
-            arrived(qo.at[t // 2, :, core], q_local.at[t // 2])
-            arrived(qo.at[t // 2, :, other], q_remote.at[t // 2])
-
-        @pl.when(t == 0)
-        def _():
-            arrived(om.at[other], meta_sem.at[0])
+        @pl.when((t + AHEAD < chunks) & (t % 2 == 0))
+        def _():
+            await_queries((t + AHEAD) // 2)
 
         for n in (2, 1, 0):
             pass_back(t, n)
@@ -446,16 +515,22 @@
         def _():
             arrived(kvo.at[:, :, core], kv_sem.at[0])
             arrived(kvo.at[:, :, other], kv_sem.at[1])
-
-        @pl.when((t < chunks) & (t % 2 == 0))
-        def _():
-            halo_out(t // 2)
-
-        ih, liveh = during(t, RELAY)
-
-        @pl.when(liveh & (ih % 2 == 0))
-        def _():
-            halo_relay(ih // 2)
+            for i in range(2):
+                pass_ahead(0, i)
+
+        for n in range(2):
+            for i in range(2):
+
+                @pl.when(t == 2 * n + 2 + i)
+                def _():
+                    pass_ahead(n + 1, i)
+
+        for lag, run in ((0, halo_out), (RELAY, halo_relay)):
+            i = t - lag
+
+            @pl.when((i >= 0) & (i < 2 * heads) & (i % 2 == 0))
+            def _():
+                run(lax.rem(i // 2 + kv_head, heads))
 
         i3, live3 = during(t, LAGS[2])
 
@@ -463,8 +538,7 @@
         def _():
             @pl.when(i3 % 2 == 0)
             def _():
-                for x in range(2):
-                    vt[i3 // 2, x] = kvo[i3 // 2, 1, x].T
+                turn_values(i3 // 2)
 
             @pl.when(has_ahead)
             def _():
@@ -483,6 +557,23 @@
             def _():
                 far(i, which)
 
+        @pl.when(t == KV_STEP)
+        def _():
+            await_queries(kv_head)
+
+            @pl.when(has_back)
+            def _():
+                for i in range(2):
+                    key_send(2, i).wait_recv()
+
+            halo_in(kv_head)
+            turn_values(kv_head)
+            turn_halo(kv_head)
+
+        @pl.when((t >= KV_STEP) & (t < KV_STEP + 2))
+        def _():
+            own_by_keys(t - KV_STEP)
+
         i6, live6 = during(t, LAGS[5])
 
         @pl.when(live6)
@@ -492,9 +583,7 @@
             @pl.when(i6 % 2 == 0)
             def _():
                 halo_in(h)
-                for direction in range(2):
-                    for x in range(2):
-                        vth[direction, x] = kvh[direction, h, 1, x].T
+                turn_halo(h)
 
             own(i6)
 
@@ -511,12 +600,15 @@
         arrived(om, x_sent.at[3])
         arrived(rm.at[0:2], x_sent.at[4])
         arrived(rm.at[2], x_sent.at[5])
-        arrived(qo, m_sent.at[0])
+        arrived(qo.at[0:kv_head], m_sent.at[0])
         arrived(rq.at[:, 0:2], m_sent.at[1])
         arrived(rq.at[:, 2], m_sent.at[2])
 
     @pl.when(has_ahead)
     def _():
+        arrived(rk.at[0], k_sent.at[0])
+        arrived(rk.at[0], k_sent.at[1])
+        arrived(rk.at[0, :, 1], k_sent.at[2])
         for which, (lo, hi) in enumerate(slots):
             arrived(so.at[:, lo:hi], n_sent.at[which])
             arrived(sl.at[:, lo:hi], l_sent.at[which])
@@ -541,7 +633,7 @@
     frames, rows, width, channels = queries.shape
     tokens = frames * rows * width
     heads = channels // HD // 2
-    chunks = 2 * heads
+    chunks = 2 * heads - 2
     half = tokens // 2
     bf16, f32 = jnp.bfloat16, jnp.float32
     dma = pltpu.SemaphoreType.DMA
@@ -565,6 +657,7 @@
             pltpu.VMEM((heads, 2, 2, half, HD), bf16),
             pltpu.VMEM((2, 8, HD), f32),
             pltpu.VMEM((5, 8, HD), f32),
+            pltpu.VMEM((3, 2, 2, tokens, HD), bf16),
             dma((heads,)),
             dma((heads,)),
             dma((2,)),
@@ -578,6 +671,8 @@
             dma((3,)),
             dma((6,)),
             dma((2,)),
+            dma((3, 2)),
+            dma((3,)),
             dma((3,)),
         ],
         compiler_params=pltpu.CompilerParams(

time: 116 us -> 107 us (0.922)
  Pallas kernels: 111 us -> 101 us
    pallas_call x1, Pallas kernels: 111 us -> 101 us  [local(): pl.pallas_call(functools.partial(kernel, blocks, tiles, heads), out_shape...]
where the time goes in v3:
time: 107 us; the launch traced here: 105 us
  Pallas kernels  101 us (94%)
  local copies, waits for them, and re-layouts  2.46 us (2%)
    pallas_call x1, Pallas kernels, local(): pl.pallas_call(functools.partial(kernel, blocks, tiles, heads), out_shape...  101 us
    unnamed x1, local copies, waits for them, and re-layouts  2.46 us

profile of v3, /device:TPU:7, one launch (start us, length us, event | category | flops | bytes accessed | tf_op | source)
XLA Modules:
  0.0 104.6 jit_solution(14023593751603404356)
XLA Ops:
  0.7 101.5 %shard_map.55 = bf16[2,128,2560]{2,1,0:T(8,128)(2,1)} custom-call(bf16[2,128,2560]{2,1,0:T(8,128)(2,1)} %bitcast.8, bf16[256,2560]{1,0:T(8,128)(2,1)} %bitcast.9, bf16[256,2560]{1,0:T(8,128)(2,1)} %bitcast.10, s32[3]{0:T(128)} %bitcast.11, s32[1]{0:T(128)} %bitcast.6.reach_ref), custom_call_target="tpu_custom_call" | custom-call | tf_op jit(solution)/shard_map/pallas_call | solution.py:640
  102.1 2.5 %copy.8 = bf16[2,2,64,2560]{3,2,1,0:T(8,128)(2,1)} copy(bf16[2,2,64,2560]{3,2,1,0:T(8,128)(2,1)} %bitcast.7) | data formatting | bytes 2621440

commit v4 on v3

--- a/solution.py
+++ b/solution.py
@@ -12,9 +12,10 @@
 BIG = 1e30
 SCALE = math.log2(math.e) / math.sqrt(HD)
 AHEAD = 2
-KV_STEP = 7
-LAGS = (0, 2, 3, 5, 7, 9)
-RELAY = 4
+KV_STEP = 6
+LAGS = (0,2,3,5,7,9)
+RELAY = 3
+OWN = 8
 MESH = pl.DeviceIdType.MESH
 
 
@@ -80,6 +81,10 @@
     so,
     sl,
     outs,
+    fp,
+    fl,
+    op,
+    ol,
     om,
     rm,
     rk,
@@ -141,9 +146,22 @@
         return pl.ds(pl.multiple_of((half * heads + h) * HD, HD), HD)
 
     barrier = pltpu.get_barrier_semaphore()
-    rings = ({"tile": lax.rem(tile + 1, tiles)}, {"tile": lax.rem(tile + tiles - 1, tiles)})
-    for device in (partner, back, ahead) + rings:
-        pl.semaphore_signal(barrier, inc=1, device_id=device, device_id_type=MESH)
+    pl.semaphore_signal(barrier, inc=1, device_id=partner, device_id_type=MESH)
+    beside = (
+        (has_back, back),
+        (has_ahead, ahead),
+        (has_up, {"tile": lax.max(tile - 1, 0)}),
+        (has_down, {"tile": lax.min(tile + 1, tiles - 1)}),
+    )
+    peers = 1
+    for there, device in beside:
+        peers = peers + jnp.where(there, 1, 0)
+
+        @pl.when(there)
+        def _():
+            pl.semaphore_signal(barrier, inc=1, device_id=device, device_id_type=MESH)
+
+    peers = peers + jnp.where(detours | relays, 2, 0)
 
     @pl.when(detours)
     def _():
@@ -207,13 +225,7 @@
             for i in range(2):
                 rk[n, i] = jnp.zeros(rk.shape[2:], rk.dtype)
 
-    @pl.when(detours | relays)
-    def _():
-        pl.semaphore_wait(barrier, 7)
-
-    @pl.when(jnp.logical_not(detours | relays))
-    def _():
-        pl.semaphore_wait(barrier, 5)
+    pl.semaphore_wait(barrier, peers)
 
     remote(om.at[core], om.at[core], x_sent.at[0], meta_sem.at[0], partner).start()
 
@@ -352,38 +364,47 @@
             for copy in out_send(which, i):
                 copy.wait_recv()
 
-    def far(i, which):
-        lo, hi = slots[which]
+    def far(i, lo, hi):
         h = i // 2
-        width = (hi - lo) * HD
-        queries = rq[i, lo:hi].reshape(width, HD)
-        seen = []
-        for side in (2, 1):
-            flags = [rm[j, j + side : j + side + 1, :] > 0.5 for j in range(lo, hi)]
-            seen.append(jnp.concatenate([jnp.where(f, 1.0, 0.0) for f in flags], axis=1) > 0.5)
+        queries = rq[i, lo:hi].reshape((hi - lo) * HD, HD)
         parts = []
         for x in range(2):
+            side = 2 - x
+            flags = [jnp.where(rm[j, j + side : j + side + 1, :] > 0.5, 1.0, 0.0) for j in range(lo, hi)]
+            seen = (flags[0] if len(flags) == 1 else jnp.concatenate(flags, axis=1)) > 0.5
             scores = scores_of(kvo[h, 0, x], queries)
-            parts.append((scores, vt[h, x], [(0, scores.shape[0], seen[x])]))
+            parts.append((scores, vt[h, x], [(0, scores.shape[0], seen)]))
         out, total, top = attend(parts)
         lse, scale = settle(total, top)
-        if which:
-            join(which - 1, i)
+        out = out * scale
         for n, j in enumerate(range(lo, hi)):
             lanes = slice(n * HD, (n + 1) * HD)
-            part, own_lse, own_scale = out[:, lanes], lse[:, lanes], scale[:, lanes]
-            if which:
-                wa, wb, new_lse = merge(own_lse, rl[i, j + 2])
-                part = part * (own_scale * wa) + ro[i, j + 2].astype(jnp.float32) * wb
-                own_lse = new_lse
-            else:
-                part = part * own_scale
-            so[i, j] = part.astype(jnp.bfloat16)
-            sl[i, j] = own_lse
+            yield j, out[:, lanes], lse[:, lanes]
+
+    def send_ahead(i, which):
         @pl.when(has_ahead)
         def _():
             for copy in out_send(which, i):
                 copy.start()
+
+    def far_first(i):
+        for j, part, lse in far(i, *slots[0]):
+            so[i, j] = part.astype(jnp.bfloat16)
+            sl[i, j] = lse
+        send_ahead(i, 0)
+        for which in (1, 2):
+            for j, part, lse in far(i, *slots[which]):
+                fp[i, j] = part
+                fl[i, j] = lse
+
+    def far_join(i, which):
+        join(which - 1, i)
+        for j in range(*slots[which]):
+            wa, wb, lse = merge(fl[i, j], rl[i, j + 2])
+            part = fp[i, j] * wa + ro[i, j + 2].astype(jnp.float32) * wb
+            so[i, j] = part.astype(jnp.bfloat16)
+            sl[i, j] = lse
+        send_ahead(i, which)
 
     def near(h, f, x):
         queries = qo[h, f, x]
@@ -421,16 +442,21 @@
             partner,
         ).start()
 
-    def own(i):
+    def own_first(i):
         h, f = i // 2, i % 2
         for x in range(2):
             _, parts = near(h, f, x)
             out, total, top = attend(parts)
             lse, scale = settle(total, top)
-            if x == 0:
-                join(2, i)
-            wa, wb, _ = merge(lse, rl[i, x])
-            whole = out * (scale * wa) + ro[i, x].astype(jnp.float32) * wb
+            op[i, x] = out * scale
+            ol[i, x] = lse
+
+    def own_join(i):
+        h, f = i // 2, i % 2
+        join(2, i)
+        for x in range(2):
+            wa, wb, _ = merge(ol[i, x], rl[i, x])
+            whole = op[i, x] * wa + ro[i, x].astype(jnp.float32) * wb
             outs[h, f, x] = whole.T.astype(jnp.bfloat16)
         give_out(h, f)
 
@@ -525,12 +551,15 @@
                 def _():
                     pass_ahead(n + 1, i)
 
-        for lag, run in ((0, halo_out), (RELAY, halo_relay)):
-            i = t - lag
-
-            @pl.when((i >= 0) & (i < 2 * heads) & (i % 2 == 0))
-            def _():
-                run(lax.rem(i // 2 + kv_head, heads))
+        @pl.when(t < heads)
+        def _():
+            halo_out(lax.rem(t + kv_head, heads))
+
+        i = t - RELAY
+
+        @pl.when((i >= 0) & (i < 2 * heads) & (i % 2 == 0))
+        def _():
+            halo_relay(lax.rem(i // 2 + kv_head, heads))
 
         i3, live3 = during(t, LAGS[2])
 
@@ -548,14 +577,7 @@
                 def _():
                     meta_send(2).wait_recv()
 
-            far(i3, 0)
-
-        for which in (1, 2):
-            i, live = during(t, LAGS[2 + which])
-
-            @pl.when(live)
-            def _():
-                far(i, which)
+            far_first(i3)
 
         @pl.when(t == KV_STEP)
         def _():
@@ -574,18 +596,29 @@
         def _():
             own_by_keys(t - KV_STEP)
 
+        i, live = during(t, OWN)
+
+        @pl.when(live)
+        def _():
+            @pl.when(i % 2 == 0)
+            def _():
+                halo_in(i // 2)
+                turn_halo(i // 2)
+
+            own_first(i)
+
+        for which in (1, 2):
+            i, live = during(t, LAGS[2 + which])
+
+            @pl.when(live)
+            def _():
+                far_join(i, which)
+
         i6, live6 = during(t, LAGS[5])
 
         @pl.when(live6)
         def _():
-            h = i6 // 2
-
-            @pl.when(i6 % 2 == 0)
-            def _():
-                halo_in(h)
-                turn_halo(h)
-
-            own(i6)
+            own_join(i6)
 
         return 0
 
@@ -655,6 +688,10 @@
             pltpu.VMEM((chunks, 5, HD, half), bf16),
             pltpu.VMEM((chunks, 5, 1, half), f32),
             pltpu.VMEM((heads, 2, 2, half, HD), bf16),
+            pltpu.VMEM((chunks, 3, HD, half), f32),
+            pltpu.VMEM((chunks, 3, 1, half), f32),
+            pltpu.VMEM((chunks, 2, HD, half), f32),
+            pltpu.VMEM((chunks, 2, 1, half), f32),
             pltpu.VMEM((2, 8, HD), f32),
             pltpu.VMEM((5, 8, HD), f32),
             pltpu.VMEM((3, 2, 2, tokens, HD), bf16),
@@ -676,7 +713,7 @@
             dma((3,)),
         ],
         compiler_params=pltpu.CompilerParams(
-            collective_id=0, has_side_effects=True, vmem_limit_bytes=62 * 1024 * 1024
+            collective_id=0, has_side_effects=True, vmem_limit_bytes=52 * 1024 * 1024
         ),
     )(
         queries.reshape(2, half, channels),

time: 107 us -> 104 us (0.972); the launches traced: 105 us -> 104 us
    unnamed x1 -> x3, local copies, waits for them, and re-layouts: 2.46 us -> 1.71 us
where the time goes in v4:
time: 104 us
  Pallas kernels  101 us (97%)
  local copies, waits for them, and re-layouts  1.71 us (2%)
    pallas_call x1, Pallas kernels, local(): pl.pallas_call(functools.partial(kernel, blocks, tiles, heads), out_shape...  101 us

profile of v4, /device:TPU:7, one launch (start us, length us, event | category | flops | bytes accessed | tf_op | source)
XLA Modules:
  0.0 103.6 jit_solution(3296331363662043571)
XLA Ops:
  0.7 0.0 copy-start
  0.7 0.6 copy-done
  1.3 101.2 %shard_map.55 = bf16[2,128,2560]{2,1,0:T(8,128)(2,1)S(1)} custom-call(bf16[2,128,2560]{2,1,0:T(8,128)(2,1)} %bitcast.9, bf16[256,2560]{1,0:T(8,128)(2,1)} %bitcast.10, bf16[256,2560]{1,0:T(8,128)(2,1)} %bitcast.11, s32[3]{0:T(128)S(1)} %bitcast.8, s32[1]{0:T(128)} %bitcast.6.reach_ref), custom_call_target="tpu_custom_call" | custom-call | tf_op jit(solution)/shard_map/pallas_call | solution.py:673
  102.5 1.1 %copy.8 = bf16[2,2,64,2560]{3,2,1,0:T(8,128)(2,1)} copy(bf16[2,2,64,2560]{3,2,1,0:T(8,128)(2,1)S(1)} %bitcast.7) | data formatting | bytes 2621440
Async XLA Ops:
  0.7 0.7 copy-start
